TPU v7x, 512 devices: a whole 4x4x16 slice. The times are simulated.
512 devices in a mesh: row: 16 (over y_hi, x, core), col: 32 (over z, y_lo).
Axes of the slice: x: 4, y: 4 (y_hi: 2, y_lo: 2; y = y_hi * 2 + y_lo), z: 16, core: 2. Of those that a mesh axis runs over, the one named last changes fastest.
Arguments:
- specimen: float32 [2, 2048, 8192], P(None, 'row', 'col'), may hold values from -6 to 6
- probe_field: float32 [2, 256, 256], replicated, may hold values from -6 to 6
- scan_offsets: int32 [16, 32, 2, 2], replicated, may hold values from -128 to 128, as said below
- live_counts: int32 [16, 32], replicated, may hold values from 1 to 2, as said below
- magnitudes: float32 [16, 32, 2, 256, 256], P('row', 'col'), may hold values from 0 to 2
Outputs:
- specimen_next: float32 [2, 2048, 8192], P(None, 'row', 'col')
- probe_next: float32 [2, 256, 256], replicated
Inputs may be any that keep to these rules, and one draw needn't show every extreme that they name: `scan_offsets`: rows of a patch start within -128 to 0 of the tile's first row, columns within -128 to 128 of its first column. Tile (a, b) owns the positions in its first live_counts[a, b] slots.
All inputs are finite; a program needn't handle non-finite values.
Results may differ from a plain program's by a relative error of at most 0.0003.
Values sent between devices are 32-bit elements; how exact they have to be, the bound alone decides.
A program may use at most 64 MiB of HBM per device.

v0:
```python
import math
import jax
import jax.numpy as jnp
from jax import lax
from jax.sharding import PartitionSpec as P

modulus_floor = 0.25
object_damping = 0.1
probe_damping = 0.1


def extended_2(block, sides, width):
    for axis, dim in sides:
        count = lax.axis_size(axis)
        forward = [(i, i + 1) for i in range(count - 1)]
        backward = [(target, source) for source, target in forward]
        low = lax.ppermute(
            lax.slice_in_dim(block, block.shape[dim] - width, None, axis=dim), axis, forward
        )
        high = lax.ppermute(lax.slice_in_dim(block, 0, width, axis=dim), axis, backward)
        block = jnp.concatenate([low, block, high], axis=dim)
    return block


def dft_tables(width):
    counter = jnp.arange(width, dtype=jnp.int32)
    phase = counter[:, None] * counter[None, :] % width
    angle = phase.astype(jnp.float32) * (2.0 * math.pi / width)
    factor = 1.0 / math.sqrt(width)
    return (jnp.cos(angle) * factor, jnp.sin(angle) * factor)


def matmul_right(left, table):
    return jnp.einsum("sjm,ml->sjl", left, table, precision=lax.Precision.HIGHEST)


def matmul_left(table, right):
    return jnp.einsum("kj,sjl->skl", table, right, precision=lax.Precision.HIGHEST)


def transform(wave_real, wave_imag, cosine, sine, direction):
    inner_real = matmul_right(wave_real, cosine) + direction * matmul_right(wave_imag, sine)
    inner_imag = matmul_right(wave_imag, cosine) - direction * matmul_right(wave_real, sine)
    outer_real = matmul_left(cosine, inner_real) + direction * matmul_left(sine, inner_imag)
    outer_imag = matmul_left(cosine, inner_imag) - direction * matmul_left(sine, inner_real)
    return (outer_real, outer_imag)


def fold_rims(wide, tile_r, tile_c, half):
    center = wide[:, 2 * half : 2 * half + tile_r, :]
    center = center.at[:, :half, :].add(wide[:, :half, :])
    center = center.at[:, tile_r - half :, :].add(wide[:, tile_r + 3 * half :, :])
    result = center[:, :, 2 * half : 2 * half + tile_c]
    result = result.at[:, :, :half].add(center[:, :, :half])
    result = result.at[:, :, tile_c - half :].add(center[:, :, tile_c + 3 * half :])
    return result


def shards(specimen, probe_field, scan_offsets, live_counts, magnitudes):
    width = probe_field.shape[1]
    half = width // 2
    tile_r = specimen.shape[1]
    tile_c = specimen.shape[2]
    slots = magnitudes.shape[2]
    row_place = lax.axis_index("row")
    col_place = lax.axis_index("col")
    zero_index = jnp.zeros((), jnp.int32)
    extended = extended_2(specimen, (("row", 1), ("col", 2)), half)
    offsets_here = scan_offsets[row_place, col_place]
    live = (jnp.arange(slots, dtype=jnp.int32) < live_counts[row_place, col_place]).astype(
        jnp.float32
    )[:, None, None]
    row_starts = offsets_here[:, 0] + half
    col_starts = offsets_here[:, 1] + half

    def extract(row_start, col_start):
        return lax.dynamic_slice(extended, (zero_index, row_start, col_start), (2, width, width))

    patches = jax.vmap(extract)(row_starts, col_starts)
    patch_real = patches[:, 0]
    patch_imag = patches[:, 1]
    probe_real = probe_field[0]
    probe_imag = probe_field[1]
    power = probe_real * probe_real + probe_imag * probe_imag
    cosine, sine = dft_tables(width)
    wave_real = probe_real * patch_real - probe_imag * patch_imag
    wave_imag = probe_real * patch_imag + probe_imag * patch_real
    far_real, far_imag = transform(wave_real, wave_imag, cosine, sine, 1.0)
    modulus = jnp.sqrt(far_real * far_real + far_imag * far_imag)
    factor = magnitudes[0, 0] / jnp.maximum(modulus, modulus_floor) - 1.0
    diff_real, diff_imag = transform(far_real * factor, far_imag * factor, cosine, sine, -1.0)
    diff_real = diff_real * live
    diff_imag = diff_imag * live
    grad_real = probe_real * diff_real + probe_imag * diff_imag
    grad_imag = probe_real * diff_imag - probe_imag * diff_real
    pieces = jnp.stack([grad_real, grad_imag, live * power], axis=1)
    layers = pieces.shape[1]

    def place(slot, total):
        start = (zero_index, row_starts[slot], col_starts[slot])
        current = lax.dynamic_slice(total, start, (layers, width, width))
        return lax.dynamic_update_slice(total, current + pieces[slot], start)

    start_total = jnp.zeros((layers, tile_r + 2 * half, tile_c + 2 * half), jnp.float32)
    buffer = lax.fori_loop(0, slots, place, start_total)
    wide = extended_2(buffer, (("row", 1), ("col", 2)), half)
    folded = fold_rims(wide, tile_r, tile_c, half)
    update = folded[:2]
    lighting = folded[2]
    damping = object_damping * jnp.max(power)
    specimen_next = specimen + update / (lighting + damping)
    local_terms = (
        jnp.sum(patch_real * diff_real + patch_imag * diff_imag, 0),
        jnp.sum(patch_real * diff_imag - patch_imag * diff_real, 0),
        jnp.sum(live * (patch_real * patch_real + patch_imag * patch_imag), 0),
    )
    sum_real, sum_imag, weight = lax.psum(
        (local_terms[0], local_terms[1], local_terms[2]), ("row", "col")
    )
    denominator = weight + probe_damping * jnp.mean(weight)
    probe_next = probe_field + jnp.stack([sum_real, sum_imag]) / denominator
    return (specimen_next, probe_next)


def solution(mesh):
    return jax.shard_map(
        shards,
        mesh=mesh,
        in_specs=(P(None, "row", "col"), P(), P(), P(), P("row", "col", None, None, None)),
        out_specs=(P(None, "row", "col"), P()),
        check_vma=False,
    )
```

profile of v0, /device:TPU:8, one launch (start us, length us, event | category | flops | bytes accessed | tf_op | source)
XLA Modules:
  0.0 654.2 jit_solution(3833202811847272772)
XLA Ops:
  7.2 1.9 collective-permute-start
  15.0 3.7 collective-permute-start.2
  18.7 4.1 collective-permute-start.3
  24.7 13.0 %collective-permute-done.2 = f32[2,384,128]{2,1,0:T(8,128)S(1)} collective-permute-done((f32[2,384,128]{2,1,0:T(8,128)}, f32[2,384,128]{2,1,0:T(8,128)S(1)}, u32[]{:S(2)}, u32[]{:S(2)}) %collective-permute-start.2) | collective-permute-done | bytes 393248 | tf_op jit(solution)/shard_map/ppermute | solution.py:17
  39.7 5.8 while.21
  40.4 2.3 bitcast_dynamic-update-slice_fusion.2
  43.3 2.2 bitcast_dynamic-update-slice_fusion.2
  45.6 2.9 fusion.49
  55.1 1.8 fusion.51
  56.9 2.0 fusion.8
  58.9 2.0 fusion.25
  69.1 2.6 fusion.39
  71.7 2.4 fusion.4
  75.3 4.0 fusion.16
  80.8 34.3 %while.20 = (s32[]{:T(128)}, f32[3,384,512]{2,1,0:T(8,128)S(1)}, s32[2]{0:T(128)S(1)}, s32[2]{0:T(128)S(1)}, f32[2,3,256,256]{3,2,0,1:T(8,128)}, /*index=5*/s32[]{:T(128)}, s32[]{:T(128)}, s32[]{:T(128)}, s32[]{:T(128)}) while((s32[]{:T(128)}, f32[3,384,512]{2,1,0:T(8,128)S(1)}, s32[2]{0:T(128)S(1)}, s32[2]{0:T(128)S(1)}, ...), condition=%wide.region_1.2_spmd, body=%wide.region_0.1_spmd.sunk | while | flops 196616 | bytes 3932361 | solution.py:105
  87.4 10.8 %dynamic_update_slice.8 = f32[3,384,512]{2,1,0:T(8,128)S(1)} dynamic-update-slice(f32[3,384,512]{2,1,0:T(8,128)S(1)} %get-tuple-element.311, f32[3,256,256]{2,1,0:T(8,128)S(1)} %bitcast_add_fusion.2, s32[]{:T(128)} %constant.194.clone.1..sunk, s32[]{:T(128)S(6)} %select_n.146, s32[]{:T(128)S(6)} %select_n.147) | dynamic-update-slice | bytes 1572868 | tf_op jit(solution)/shard_map/while/body/eval_jaxpr/dynamic_update_slice | solution.py:102
  104.8 10.4 %dynamic_update_slice.8 = f32[3,384,512]{2,1,0:T(8,128)S(1)} dynamic-update-slice(f32[3,384,512]{2,1,0:T(8,128)S(1)} %get-tuple-element.311, f32[3,256,256]{2,1,0:T(8,128)S(1)} %bitcast_add_fusion.2, s32[]{:T(128)} %constant.194.clone.1..sunk, s32[]{:T(128)S(6)} %select_n.146, s32[]{:T(128)S(6)} %select_n.147) | dynamic-update-slice | bytes 1572868 | tf_op jit(solution)/shard_map/while/body/eval_jaxpr/dynamic_update_slice | solution.py:102
  115.3 8.6 %collective-permute-start.4 = (f32[3,128,512]{2,1,0:T(8,128)S(1)}, f32[3,128,512]{2,1,0:T(8,128)S(1)}, u32[]{:S(2)}, u32[]{:S(2)}) collective-permute-start(f32[3,128,512]{2,1,0:T(8,128)S(1)} %get-tuple-element.210), channel_id=1, source_target_pairs={{0,32},{32,64},{64,96},{96,128},{128,160},{160,192},{192,224},{224... | collective-permute-start | bytes 2359304 | tf_op jit(solution)/shard_map/ppermute | solution.py:17
  126.1 3.6 collective-permute-done.5
  131.9 2.4 collective-permute-start.6
  134.3 3.5 collective-permute-start.7
  139.3 498.2 %all-reduce.3.cloned.1.call-done = (f32[1,256,256]{2,1,0:T(8,128)}, f32[1,256,256]{2,1,0:T(8,128)}, f32[256,256]{1,0:T(8,128)}) async-done(((f32[1,256,256]{2,1,0:T(8,128)}, f32[1,256,256]{2,1,0:T(8,128)}, f32[256,256]{1,0:T(8,128)}), (f32[1,256,256]{2,1,0:T(8,128)}, f32[1,256,256]{2,1,0:T(8,128)}, f32[256,256]{1,0:T(8,128)})) %all-reduce.3.cloned.1.call-update) | async-done | bytes 786448 | tf_op jit(solution)/shard_map/psum | solution.py:117
  640.8 1.9 fusion.10
  642.7 1.9 fusion.9
  (80 shorter events, 44.6 us)
Async XLA Ops:
  7.2 4.4 copy-start
  7.2 6.1 copy-start.5
  7.2 630.3 %all-reduce.3.cloned.1.call-start = ((), (), s32[]{:S(2)}) async-start(), calls=%async_computation | async-start | bytes 1572864 | tf_op jit(solution)/shard_map/psum | solution.py:117
  7.2 6.0 collective-permute-start
  9.1 4.9 collective-permute-start.1
  13.2 10.3 %copy-start.7 = (f32[1,1,2,256,256]{4,3,2,1,0:T(8,128)S(1)}, f32[1,1,2,256,256]{4,3,2,1,0:T(8,128)}, u32[]{:S(2)}) copy-start(f32[1,1,2,256,256]{4,3,2,1,0:T(8,128)} %param.23) | copy-start | bytes 1572868
  15.0 22.7 %collective-permute-start.2 = (f32[2,384,128]{2,1,0:T(8,128)}, f32[2,384,128]{2,1,0:T(8,128)S(1)}, u32[]{:S(2)}, u32[]{:S(2)}) collective-permute-start(f32[2,384,128]{2,1,0:T(8,128)} %get-tuple-element.217), channel_id=1, source_target_pairs={{0,1},{1,2},{2,3},{3,4},{4,5},{5,6},{6,7},{7,8},{8,9},{9,10},{10,1... | collective-permute-start | bytes 1179656 | tf_op jit(solution)/shard_map/ppermute | solution.py:17
  18.7 19.7 %collective-permute-start.3 = (f32[2,384,128]{2,1,0:T(8,128)}, f32[2,384,128]{2,1,0:T(8,128)}, u32[]{:S(2)}, u32[]{:S(2)}) collective-permute-start(f32[2,384,128]{2,1,0:T(8,128)} %get-tuple-element.218), channel_id=1, source_target_pairs={{1,0},{2,1},{3,2},{4,3},{5,4},{6,5},{7,6},{8,7},{9,8},{10,9},{11,1... | collective-permute-start | bytes 1179656 | tf_op jit(solution)/shard_map/ppermute | solution.py:20
  37.7 0.8 copy-start.9
  45.6 2.9 copy-start.4
  55.1 3.8 copy-start.8
  115.3 10.5 %collective-permute-start.4 = (f32[3,128,512]{2,1,0:T(8,128)S(1)}, f32[3,128,512]{2,1,0:T(8,128)S(1)}, u32[]{:S(2)}, u32[]{:S(2)}) collective-permute-start(f32[3,128,512]{2,1,0:T(8,128)S(1)} %get-tuple-element.210), channel_id=1, source_target_pairs={{0,32},{32,64},{64,96},{96,128},{128,160},{160,192},{192,224},{224... | collective-permute-start | bytes 2359304 | tf_op jit(solution)/shard_map/ppermute | solution.py:17
  124.0 5.7 collective-permute-start.5
  129.7 2.2 copy-start.1
  129.7 8.1 %copy-start.3 = (f32[2,256,256]{2,1,0:T(8,128)S(1)}, f32[2,256,256]{2,1,0:T(8,128)}, u32[]{:S(2)}) copy-start(f32[2,256,256]{2,1,0:T(8,128)} %param.20) | copy-start | bytes 1572868
  131.9 510.8 %collective-permute-start.6 = (f32[3,640,128]{2,1,0:T(8,128)}, f32[3,640,128]{2,1,0:T(8,128)S(1)}, u32[]{:S(2)}, u32[]{:S(2)}) collective-permute-start(f32[3,640,128]{2,1,0:T(8,128)} %get-tuple-element.207), channel_id=1, source_target_pairs={{0,1},{1,2},{2,3},{3,4},{4,5},{5,6},{6,7},{7,8},{8,9},{9,10},{10,1... | collective-permute-start | bytes 2949128 | tf_op jit(solution)/shard_map/ppermute | solution.py:17
  134.3 508.4 %collective-permute-start.7 = (f32[3,640,128]{2,1,0:T(8,128)S(1)}, f32[3,640,128]{2,1,0:T(8,128)S(1)}, u32[]{:S(2)}, u32[]{:S(2)}) collective-permute-start(f32[3,640,128]{2,1,0:T(8,128)S(1)} %get-tuple-element.208), channel_id=1, source_target_pairs={{1,0},{2,1},{3,2},{4,3},{5,4},{6,5},{7,6},{8,7},{9,8},{10,9},{11,1... | collective-permute-start | bytes 2949128 | tf_op jit(solution)/shard_map/ppermute | solution.py:20
  642.7 2.8 copy-start.2
  645.6 1.0 copy-start.6
Sparse Core Ops, SparseCore 0:
  138.0 499.5 all-reduce.2
where the time goes:
time: 655 us; the launch traced here: 654 us
  waiting for transfers between devices  516 us (79%)
  local copies, waits for them, and re-layouts  39.8 us (6%)
  matrix products  32.3 us (5%)
  starting transfers between devices  26.8 us (4%)
  between operations  15.8 us (2%)
  other arithmetic  15.6 us (2%)
  loops' own time  7.67 us (1%)
    psum x1, waiting for transfers between devices, shards(): lax.psum((local_terms[0], local_terms[1], local_terms[2]), ('row', 'col'))  498 us
    dynamic_update_slice x2, local copies, waits for them, and re-layouts, place(): return lax.dynamic_update_slice(total, current + pieces[slot], start)  21.2 us
    dot_general x8, matrix products, matmul_left(): jnp.einsum('kj,sjl->skl', table, right, precision=lax.Precision.HIGHEST)  18.1 us
    ppermute x4, starting transfers between devices, extended_2(): lax.ppermute(lax.slice_in_dim(block, block.shape[dim] - width, None, axis...  16.6 us
    dot_general x8, matrix products, matmul_right(): jnp.einsum('sjm,ml->sjl', left, table, precision=lax.Precision.HIGHEST)  14.2 us
    ppermute x4, waiting for transfers between devices, extended_2(): lax.ppermute(lax.slice_in_dim(block, block.shape[dim] - width, None, axis...  13.5 us
  transfers between devices with their start and end apart: 9, of which 5 were waited for; matrix products, arithmetic and copies ran while one was open for 2% of the time, Pallas kernels for 0%

commit v1 on v0

--- a/solution.py
+++ b/solution.py
@@ -115,7 +115,7 @@
         jnp.sum(live * (patch_real * patch_real + patch_imag * patch_imag), 0),
     )
     sum_real, sum_imag, weight = lax.psum(
-        (local_terms[0], local_terms[1], local_terms[2]), ("row", "col")
+        lax.psum((local_terms[0], local_terms[1], local_terms[2]), "row"), "col"
     )
     denominator = weight + probe_damping * jnp.mean(weight)
     probe_next = probe_field + jnp.stack([sum_real, sum_imag]) / denominator

time: 655 us -> 582 us (0.89)
  the two profiles are of different devices: /device:TPU:8 before, /device:TPU:2 now
where the time goes in v1:
time: 582 us; the launch traced here: 581 us
  waiting for transfers between devices  444 us (76%)
  local copies, waits for them, and re-layouts  43 us (7%)
  matrix products  32.4 us (6%)
  starting transfers between devices  21.5 us (4%)
  between operations  15.8 us (3%)
  other arithmetic  15.5 us (3%)
  loops' own time  8.34 us (1%)
    psum x1, waiting for transfers between devices, shards(): lax.psum(lax.psum((local_terms[0], local_terms[1], local_terms[2]), 'row'...  275 us
    psum x1, waiting for transfers between devices, shards(): lax.psum((local_terms[0], local_terms[1], local_terms[2]), 'row')  154 us
    dynamic_update_slice x2, local copies, waits for them, and re-layouts, place(): return lax.dynamic_update_slice(total, current + pieces[slot], start)  22.2 us
    dot_general x8, matrix products, matmul_left(): jnp.einsum('kj,sjl->skl', table, right, precision=lax.Precision.HIGHEST)  18.1 us
    ppermute x4, waiting for transfers between devices, extended_2(): lax.ppermute(lax.slice_in_dim(block, block.shape[dim] - width, None, axis...  14.4 us
    dot_general x8, matrix products, matmul_right(): jnp.einsum('sjm,ml->sjl', left, table, precision=lax.Precision.HIGHEST)  14.3 us
    ppermute x4, starting transfers between devices, extended_2(): lax.ppermute(lax.slice_in_dim(block, block.shape[dim] - width, None, axis...  13.3 us
  transfers between devices with their start and end apart: 10, of which 4 were waited for; matrix products, arithmetic and copies ran while one was open for 2% of the time, Pallas kernels for 0%

profile of v1, /device:TPU:2, one launch (start us, length us, event | category | flops | bytes accessed | tf_op | source)
XLA Modules:
  0.0 580.7 jit_solution(17430204740772220607)
XLA Ops:
  7.2 2.1 collective-permute-start
  9.3 3.6 collective-permute-start.1
  18.1 3.5 collective-permute-start.2
  24.8 14.3 %collective-permute-done.2 = f32[2,384,128]{2,1,0:T(8,128)S(1)} collective-permute-done((f32[2,384,128]{2,1,0:T(8,128)}, f32[2,384,128]{2,1,0:T(8,128)S(1)}, u32[]{:S(2)}, u32[]{:S(2)}) %collective-permute-start.2) | collective-permute-done | bytes 393248 | tf_op jit(solution)/shard_map/ppermute | solution.py:17
  41.2 5.7 while.21
  41.9 2.2 bitcast_dynamic-update-slice_fusion.2
  44.7 2.2 bitcast_dynamic-update-slice_fusion.2
  46.9 2.9 fusion.49
  54.6 1.8 fusion.51
  58.3 2.0 fusion.8
  60.3 2.0 fusion.25
  70.5 2.6 fusion.39
  73.1 2.4 fusion.4
  76.7 4.0 fusion.16
  82.2 36.0 %while.20 = (s32[]{:T(128)}, f32[3,384,512]{2,1,0:T(8,128)S(1)}, s32[2]{0:T(128)S(1)}, s32[2]{0:T(128)S(1)}, f32[2,3,256,256]{3,2,0,1:T(8,128)}, /*index=5*/s32[]{:T(128)}, s32[]{:T(128)}, s32[]{:T(128)}, s32[]{:T(128)}) while((s32[]{:T(128)}, f32[3,384,512]{2,1,0:T(8,128)S(1)}, s32[2]{0:T(128)S(1)}, s32[2]{0:T(128)S(1)}, ...), condition=%wide.region_1.2_spmd, body=%wide.region_0.1_spmd.sunk | while | flops 196616 | bytes 3932361 | solution.py:105
  89.2 10.4 %dynamic_update_slice.8 = f32[3,384,512]{2,1,0:T(8,128)S(1)} dynamic-update-slice(f32[3,384,512]{2,1,0:T(8,128)S(1)} %get-tuple-element.314, f32[3,256,256]{2,1,0:T(8,128)S(1)} %bitcast_add_fusion.2, s32[]{:T(128)} %constant.194.clone.1..sunk, s32[]{:T(128)S(6)} %select_n.146, s32[]{:T(128)S(6)} %select_n.147) | dynamic-update-slice | bytes 1572868 | tf_op jit(solution)/shard_map/while/body/eval_jaxpr/dynamic_update_slice | solution.py:102
  106.4 11.8 %dynamic_update_slice.8 = f32[3,384,512]{2,1,0:T(8,128)S(1)} dynamic-update-slice(f32[3,384,512]{2,1,0:T(8,128)S(1)} %get-tuple-element.314, f32[3,256,256]{2,1,0:T(8,128)S(1)} %bitcast_add_fusion.2, s32[]{:T(128)} %constant.194.clone.1..sunk, s32[]{:T(128)S(6)} %select_n.146, s32[]{:T(128)S(6)} %select_n.147) | dynamic-update-slice | bytes 1572868 | tf_op jit(solution)/shard_map/while/body/eval_jaxpr/dynamic_update_slice | solution.py:102
  119.6 5.3 collective-permute-start.4
  124.9 1.9 collective-permute-start.5
  126.8 153.7 %all-reduce.7.cloned.1.call-done = (f32[256,256]{1,0:T(8,128)}, f32[256,256]{1,0:T(8,128)}, f32[256,256]{1,0:T(8,128)}) async-done(((f32[256,256]{1,0:T(8,128)}, f32[256,256]{1,0:T(8,128)}, f32[256,256]{1,0:T(8,128)}), (f32[256,256]{1,0:T(8,128)}, f32[256,256]{1,0:T(8,128)}, f32[256,256]{1,0:T(8,128)})) %all-reduce.7.cloned.1.call-update) | async-done | bytes 786448 | tf_op jit(solution)/shard_map/psum | solution.py:118
  284.2 2.4 collective-permute-start.6
  289.3 274.7 %all-reduce.5.cloned.1.call-done = (f32[1,256,256]{2,1,0:T(8,128)}, f32[1,256,256]{2,1,0:T(8,128)}, f32[256,256]{1,0:T(8,128)}) async-done(((f32[1,256,256]{2,1,0:T(8,128)}, f32[1,256,256]{2,1,0:T(8,128)}, f32[256,256]{1,0:T(8,128)}), (f32[1,256,256]{2,1,0:T(8,128)}, f32[1,256,256]{2,1,0:T(8,128)}, f32[256,256]{1,0:T(8,128)})) %all-reduce.5.cloned.1.call-update) | async-done | bytes 786448 | tf_op jit(solution)/shard_map/psum | solution.py:117
  567.3 1.9 fusion.10
  569.2 1.9 fusion.9
  (83 shorter events, 46.9 us)
Async XLA Ops:
  7.2 6.9 %copy-start = (s32[16,32,2,2]{1,3,2,0:T(2,128)S(1)}, s32[16,32,2,2]{1,3,2,0:T(2,128)}, u32[]{:S(2)}) copy-start(s32[16,32,2,2]{1,3,2,0:T(2,128)} %param.21) | copy-start | bytes 24580
  7.2 8.6 %copy-start.5 = (f32[2,128,256]{2,1,0:T(8,128)S(1)}, f32[2,128,256]{2,1,0:T(8,128)}, u32[]{:S(2)}) copy-start(f32[2,128,256]{2,1,0:T(8,128)} %param.19) | copy-start | bytes 786436
  7.2 273.3 %all-reduce.7.cloned.1.call-start = ((), (), s32[]{:S(2)}) async-start(), calls=%async_computation.1 | async-start | bytes 1572864 | tf_op jit(solution)/shard_map/psum | solution.py:118
  7.2 8.5 %collective-permute-start = (f32[2,128,256]{2,1,0:T(8,128)}, f32[2,128,256]{2,1,0:T(8,128)S(1)}, u32[]{:S(2)}, u32[]{:S(2)}) collective-permute-start(f32[2,128,256]{2,1,0:T(8,128)} %param.19), channel_id=1, source_target_pairs={{0,32},{32,64},{64,96},{96,128},{128,160},{160,192},{192,224},{224... | collective-permute-start | bytes 786440 | tf_op jit(solution)/shard_map/ppermute | solution.py:17
  9.3 7.8 %collective-permute-start.1 = (f32[2,128,256]{2,1,0:T(8,128)}, f32[2,128,256]{2,1,0:T(8,128)S(1)}, u32[]{:S(2)}, u32[]{:S(2)}) collective-permute-start(f32[2,128,256]{2,1,0:T(8,128)} %param.19), channel_id=1, source_target_pairs={{32,0},{64,32},{96,64},{128,96},{160,128},{192,160},{224,192},{256... | collective-permute-start | bytes 786440 | tf_op jit(solution)/shard_map/ppermute | solution.py:20
  15.7 7.9 %copy-start.7 = (f32[1,1,2,256,256]{4,3,2,1,0:T(8,128)S(1)}, f32[1,1,2,256,256]{4,3,2,1,0:T(8,128)}, u32[]{:S(2)}) copy-start(f32[1,1,2,256,256]{4,3,2,1,0:T(8,128)} %param.23) | copy-start | bytes 1572868
  18.1 21.0 %collective-permute-start.2 = (f32[2,384,128]{2,1,0:T(8,128)}, f32[2,384,128]{2,1,0:T(8,128)S(1)}, u32[]{:S(2)}, u32[]{:S(2)}) collective-permute-start(f32[2,384,128]{2,1,0:T(8,128)} %get-tuple-element.220), channel_id=1, source_target_pairs={{0,1},{1,2},{2,3},{3,4},{4,5},{5,6},{6,7},{7,8},{8,9},{9,10},{10,1... | collective-permute-start | bytes 1179656 | tf_op jit(solution)/shard_map/ppermute | solution.py:17
  21.6 18.3 %collective-permute-start.3 = (f32[2,384,128]{2,1,0:T(8,128)}, f32[2,384,128]{2,1,0:T(8,128)}, u32[]{:S(2)}, u32[]{:S(2)}) collective-permute-start(f32[2,384,128]{2,1,0:T(8,128)} %get-tuple-element.221), channel_id=1, source_target_pairs={{1,0},{2,1},{3,2},{4,3},{5,4},{6,5},{7,6},{8,7},{9,8},{10,9},{11,1... | collective-permute-start | bytes 1179656 | tf_op jit(solution)/shard_map/ppermute | solution.py:20
  39.2 0.8 copy-start.9
  46.9 2.9 copy-start.4
  56.4 3.8 copy-start.8
  118.3 445.8 %all-reduce.5.cloned.1.call-start = ((), (), s32[]{:S(2)}) async-start(), calls=%async_computation | async-start | bytes 1572864 | tf_op jit(solution)/shard_map/psum | solution.py:117
  119.6 160.9 %collective-permute-start.4 = (f32[3,128,512]{2,1,0:T(8,128)}, f32[3,128,512]{2,1,0:T(8,128)}, u32[]{:S(2)}, u32[]{:S(2)}) collective-permute-start(f32[3,128,512]{2,1,0:T(8,128)} %get-tuple-element.213), channel_id=1, source_target_pairs={{0,32},{32,64},{64,96},{96,128},{128,160},{160,192},{192,224},{224... | collective-permute-start | bytes 2359304 | tf_op jit(solution)/shard_map/ppermute | solution.py:17
  124.9 157.0 %collective-permute-start.5 = (f32[3,128,512]{2,1,0:T(8,128)}, f32[3,128,512]{2,1,0:T(8,128)S(1)}, u32[]{:S(2)}, u32[]{:S(2)}) collective-permute-start(f32[3,128,512]{2,1,0:T(8,128)} %get-tuple-element.212), channel_id=1, source_target_pairs={{32,0},{64,32},{96,64},{128,96},{160,128},{192,160},{224,192},{256... | collective-permute-start | bytes 2359304 | tf_op jit(solution)/shard_map/ppermute | solution.py:20
  282.0 2.2 copy-start.1
  282.0 5.9 %copy-start.3 = (f32[2,256,256]{2,1,0:T(8,128)S(1)}, f32[2,256,256]{2,1,0:T(8,128)}, u32[]{:S(2)}) copy-start(f32[2,256,256]{2,1,0:T(8,128)} %param.20) | copy-start | bytes 1572868
  284.2 285.0 %collective-permute-start.6 = (f32[3,640,128]{2,1,0:T(8,128)}, f32[3,640,128]{2,1,0:T(8,128)S(1)}, u32[]{:S(2)}, u32[]{:S(2)}) collective-permute-start(f32[3,640,128]{2,1,0:T(8,128)} %get-tuple-element.210), channel_id=1, source_target_pairs={{0,1},{1,2},{2,3},{3,4},{4,5},{5,6},{6,7},{7,8},{8,9},{9,10},{10,1... | collective-permute-start | bytes 2949128 | tf_op jit(solution)/shard_map/ppermute | solution.py:17
  286.7 282.5 %collective-permute-start.7 = (f32[3,640,128]{2,1,0:T(8,128)S(1)}, f32[3,640,128]{2,1,0:T(8,128)S(1)}, u32[]{:S(2)}, u32[]{:S(2)}) collective-permute-start(f32[3,640,128]{2,1,0:T(8,128)S(1)} %get-tuple-element.211), channel_id=1, source_target_pairs={{1,0},{2,1},{3,2},{4,3},{5,4},{6,5},{7,6},{8,7},{9,8},{10,9},{11,1... | collective-permute-start | bytes 2949128 | tf_op jit(solution)/shard_map/ppermute | solution.py:20
  569.2 2.8 copy-start.2
  572.1 1.0 copy-start.6
Sparse Core Ops, SparseCore 0:
  118.4 162.0 all-reduce.6
  283.6 280.3 all-reduce.4
